TPU v7x, 32 devices: a whole 2x2x4 slice. The times are simulated.
32 devices in a mesh: img: 8 (over z, x), tile: 4 (over y, core).
Axes of the slice: x: 2, y: 2, z: 4, core: 2. Of those that a mesh axis runs over, the one named last changes fastest.
Arguments:
- query: bfloat16 [8, 512, 1280], P('img', 'tile'), may hold values from -6 to 6
- keys: bfloat16 [8, 512, 1280], P('img', 'tile'), may hold values from -6 to 6
- values: bfloat16 [8, 512, 1280], P('img', 'tile'), may hold values from -6 to 6
- out_weight: bfloat16 [1280, 1280], P('tile'), may hold values from -0.15625 to 0.15625
- hidden: bfloat16 [8, 512, 1280], P('img', 'tile'), may hold values from -36 to 36
- gain: float32 [1280], replicated, may hold values from 0.5 to 1.5
- seq_grad: bfloat16 [8, 512, 5120], P('img', 'tile'), may hold values from -6 to 6
- splice_at: int32 [8, 128], P('img', 'tile'), may hold values from 0 to 511, as said below
- merged_count: int32 [8], P('img'), may hold values from 16 to 128
Outputs:
- query_grad: bfloat16 [8, 512, 1280], P('img', 'tile')
- key_grad: bfloat16 [8, 512, 1280], P('img', 'tile')
- value_grad: bfloat16 [8, 512, 1280], P('img', 'tile')
- gain_grad: float32 [1280], replicated
Inputs may be any that keep to these rules, and one draw needn't show every extreme that they name: `splice_at`: within one image the positions are distinct. The merged rows of one device (aligned blocks of 32 rows) place at most 16 rows in any one block of 128 positions of the sequence.
All inputs are finite; a program needn't handle non-finite values.
Results may differ from a plain program's by a relative error of at most 0.009.
Values may be sent and summed in bfloat16 or wider, within the bound.
No kernel may reach another device: no remote copies, remote signals or barrier semaphores. Data moves between devices by JAX's collectives and lax.ppermute only.
A program may use at most 64 MiB of HBM per device.

v0:
```python
import jax
import jax.numpy as jnp
from jax import lax
from jax.sharding import PartitionSpec as P

HEAD = 80


norm_eps = 1e-06


def splice_back(seq_grad, splice_at, merged_count, width):
    seq_rows = seq_grad[0]
    span_len = seq_rows.shape[0]
    tile_count = lax.axis_size("tile")
    my_tile = lax.axis_index("tile")
    positions = splice_at[0]
    rows_here = positions.shape[0]
    capacity = 2 * rows_here // tile_count
    owners = positions // span_len
    within = positions % span_len
    onehot = (owners[:, None] == jnp.arange(tile_count, dtype=jnp.int32)[None, :]).astype(jnp.int32)
    before = jnp.cumsum(onehot, axis=0) - onehot
    rank_in = jnp.sum(before * onehot, axis=1)
    slot_ids = owners * capacity + rank_in
    requests = jnp.full((tile_count * capacity,), -1, jnp.int32).at[slot_ids].set(within)
    requests = requests.reshape(tile_count, capacity)
    asked_for = lax.all_to_all(requests, "tile", split_axis=0, concat_axis=0, tiled=True)
    found_rows = jnp.take(seq_rows, jnp.clip(asked_for, 0, span_len - 1), axis=0)
    found_rows = jnp.where(
        (asked_for >= 0)[:, :, None], found_rows, jnp.zeros((), found_rows.dtype)
    )
    replies = lax.all_to_all(found_rows, "tile", split_axis=0, concat_axis=0, tiled=True)
    merged = replies.reshape(tile_count * capacity, -1)[slot_ids]
    live_rows = my_tile * rows_here + jnp.arange(rows_here) < merged_count[0]
    merged = jnp.where(live_rows[:, None], merged, jnp.zeros((), merged.dtype))
    return merged.reshape(-1, width)


def norm_backward(hidden, gain, patch_grad):
    values32 = hidden[0].astype(jnp.float32)
    inverse = lax.rsqrt(jnp.mean(values32 * values32, axis=-1, keepdims=True) + norm_eps)
    normed = values32 * inverse
    upstream = patch_grad.astype(jnp.float32)
    gain_part = jnp.sum(upstream * normed, axis=0)
    scaled = gain * upstream
    attn_grad = (
        inverse * (scaled - normed * jnp.mean(scaled * normed, axis=-1, keepdims=True))
    ).astype(jnp.bfloat16)
    return (attn_grad, gain_part)


def to_heads(matrix, tile_count):
    return matrix.reshape(matrix.shape[0], tile_count, -1)


def head_view(arrived):
    return arrived.reshape(arrived.shape[0], -1, HEAD)


def from_heads(result, tile_count, rows_here):
    return result.reshape(tile_count, rows_here, -1)


def attend(head_q, head_k, head_v, head_g, valid_keys):
    patches, heads_here, head_size = head_q.shape
    block = min(512, patches)
    factor = head_size ** (-0.5)
    key_live = jnp.arange(patches) < valid_keys

    def one_block(index, carried):
        grad_q, grad_k, grad_v = carried
        start = index * block
        query_block = lax.dynamic_slice_in_dim(head_q, start, block, 0)
        grads_block = lax.dynamic_slice_in_dim(head_g, start, block, 0)
        scores = (
            jnp.einsum("bhe,khe->hbk", query_block, head_k, preferred_element_type=jnp.float32)
            * factor
        )
        scores = jnp.where(key_live[None, None, :], scores, -1e30)
        largest = jnp.max(scores, axis=-1, keepdims=True)
        expons = jnp.exp(scores - largest)
        probs = expons / jnp.sum(expons, axis=-1, keepdims=True)
        low_probs = probs.astype(jnp.bfloat16)
        grad_v = grad_v + jnp.einsum(
            "hbk,bhe->khe", low_probs, grads_block, preferred_element_type=jnp.float32
        )
        dprobs = jnp.einsum("bhe,khe->hbk", grads_block, head_v, preferred_element_type=jnp.float32)
        spread = jnp.sum(probs * dprobs, axis=-1, keepdims=True)
        dscores = (probs * (dprobs - spread)).astype(jnp.bfloat16)
        block_grad = (
            jnp.einsum("hbk,khe->bhe", dscores, head_k, preferred_element_type=jnp.float32) * factor
        )
        grad_k = grad_k + jnp.einsum(
            "hbk,bhe->khe", dscores, query_block, preferred_element_type=jnp.float32
        )
        grad_q = lax.dynamic_update_slice_in_dim(grad_q, block_grad.astype(jnp.bfloat16), start, 0)
        return (grad_q, grad_k, grad_v)

    initial = (
        jnp.zeros(head_q.shape, jnp.bfloat16),
        jnp.zeros(head_q.shape, jnp.float32),
        jnp.zeros(head_q.shape, jnp.float32),
    )
    upper = patches // block
    grad_q, grad_k, grad_v = lax.fori_loop(0, upper, one_block, initial)
    return (grad_q, (grad_k * factor).astype(jnp.bfloat16), grad_v.astype(jnp.bfloat16))


def body(query, keys, values, out_weight, hidden, gain, seq_grad, splice_at, merged_count):
    tile_count = lax.axis_size("tile")
    width = query.shape[-1]
    rows_here = query.shape[1]
    head_q, head_k, head_v = (
        lax.all_to_all(
            to_heads(query[0], tile_count), "tile", split_axis=1, concat_axis=0, tiled=True
        ),
        lax.all_to_all(
            to_heads(keys[0], tile_count), "tile", split_axis=1, concat_axis=0, tiled=True
        ),
        lax.all_to_all(
            to_heads(values[0], tile_count), "tile", split_axis=1, concat_axis=0, tiled=True
        ),
    )
    patch_grad = splice_back(seq_grad, splice_at, merged_count, width)
    attn_grad, gain_part = norm_backward(hidden, gain, patch_grad)
    head_g = jnp.einsum(
        "pd,cd->pc",
        lax.all_gather(attn_grad, "tile", axis=0, tiled=True),
        out_weight,
        preferred_element_type=jnp.float32,
    ).astype(jnp.bfloat16)
    gain_grad = lax.psum(gain_part, ("img", "tile"))
    valid_keys = 4 * merged_count[0]
    grad_q, grad_k, grad_v = attend(
        head_view(head_q), head_view(head_k), head_view(head_v), head_view(head_g), valid_keys
    )
    back_q, back_k, back_v = (
        lax.all_to_all(
            from_heads(grad_q, tile_count, rows_here),
            "tile",
            split_axis=0,
            concat_axis=2,
            tiled=True,
        ),
        lax.all_to_all(
            from_heads(grad_k, tile_count, rows_here),
            "tile",
            split_axis=0,
            concat_axis=2,
            tiled=True,
        ),
        lax.all_to_all(
            from_heads(grad_v, tile_count, rows_here),
            "tile",
            split_axis=0,
            concat_axis=2,
            tiled=True,
        ),
    )
    return (back_q, back_k, back_v, gain_grad)


def solution(mesh):
    return jax.shard_map(
        body,
        mesh=mesh,
        in_specs=(
            P("img", "tile", None),
            P("img", "tile", None),
            P("img", "tile", None),
            P("tile", None),
            P("img", "tile", None),
            P(),
            P("img", "tile", None),
            P("img", "tile"),
            P("img"),
        ),
        out_specs=(P("img", "tile", None), P("img", "tile", None), P("img", "tile", None), P()),
        check_vma=False,
    )
```

profile of v0, /device:TPU:0, one launch (start us, length us, event | category | flops | bytes accessed | tf_op | source)
XLA Modules:
  0.0 160.7 jit_solution(9923148058863909714)
XLA Ops:
  10.3 4.3 %all-to-all-start.2 = ((s32[4,1,16]{2,1,0:T(1,128)}), s32[4,1,16]{2,1,0:T(1,128)S(1)}, u32[]{:S(2)}, u32[]{:S(2)}) async-start(s32[4,1,16]{2,1,0:T(1,128)} %bitcast.12), calls=%async_computation.2 | async-start | bytes 4096 | tf_op jit(solution)/shard_map/all_to_all | solution.py:28
  15.2 3.1 %all-to-all-done.2 = s32[4,1,16]{2,1,0:T(1,128)S(1)} async-done(((s32[4,1,16]{2,1,0:T(1,128)}), s32[4,1,16]{2,1,0:T(1,128)S(1)}, u32[]{:S(2)}, u32[]{:S(2)}) %all-to-all-start.2) | async-done | bytes 288 | tf_op jit(solution)/shard_map/all_to_all | solution.py:28
  20.4 3.6 %all-to-all-start.3 = ((bf16[4,16,5120]{2,1,0:T(8,128)(2,1)}), bf16[4,16,5120]{2,1,0:T(8,128)(2,1)S(1)}, u32[]{:S(2)}, u32[]{:S(2)}) async-start(bf16[4,16,5120]{2,1,0:T(8,128)(2,1)} %select_select_fusion), calls=%async_computation.3 | async-start | bytes 1310720 | tf_op jit(solution)/shard_map/all_to_all | solution.py:33
  24.4 9.7 %all-to-all-done.3 = bf16[4,16,5120]{2,1,0:T(8,128)(2,1)S(1)} async-done(((bf16[4,16,5120]{2,1,0:T(8,128)(2,1)}), bf16[4,16,5120]{2,1,0:T(8,128)(2,1)S(1)}, u32[]{:S(2)}, u32[]{:S(2)}) %all-to-all-start.3) | async-done | bytes 655392 | tf_op jit(solution)/shard_map/all_to_all | solution.py:33
  37.5 3.5 %all-to-all-start = ((bf16[128,4,320]{0,2,1:T(8,128)(2,1)}), bf16[128,4,320]{0,2,1:T(8,128)(2,1)S(1)}, u32[]{:S(2)}, u32[]{:S(2)}) async-start(bf16[128,4,320]{0,2,1:T(8,128)(2,1)} %bitcast.1), calls=%async_computation | async-start | bytes 655360 | tf_op jit(solution)/shard_map/all_to_all | solution.py:115
  41.8 6.7 %all-to-all-done = bf16[128,4,320]{0,2,1:T(8,128)(2,1)S(1)} async-done(((bf16[128,4,320]{0,2,1:T(8,128)(2,1)}), bf16[128,4,320]{0,2,1:T(8,128)(2,1)S(1)}, u32[]{:S(2)}, u32[]{:S(2)}) %all-to-all-start) | async-done | bytes 327712 | tf_op jit(solution)/shard_map/all_to_all | solution.py:115
  48.5 3.5 %all-to-all-start.1 = ((bf16[128,4,320]{0,2,1:T(8,128)(2,1)}), bf16[128,4,320]{0,2,1:T(8,128)(2,1)S(1)}, u32[]{:S(2)}, u32[]{:S(2)}) async-start(bf16[128,4,320]{0,2,1:T(8,128)(2,1)} %bitcast.4), calls=%async_computation.1 | async-start | bytes 655360 | tf_op jit(solution)/shard_map/all_to_all | solution.py:118
  52.9 5.8 %all-to-all-done.1 = bf16[128,4,320]{0,2,1:T(8,128)(2,1)S(1)} async-done(((bf16[128,4,320]{0,2,1:T(8,128)(2,1)}), bf16[128,4,320]{0,2,1:T(8,128)(2,1)S(1)}, u32[]{:S(2)}, u32[]{:S(2)}) %all-to-all-start.1) | async-done | bytes 327712 | tf_op jit(solution)/shard_map/all_to_all | solution.py:118
  58.7 3.5 %all-to-all-start.4 = ((bf16[128,4,320]{0,2,1:T(8,128)(2,1)}), bf16[128,4,320]{0,2,1:T(8,128)(2,1)S(1)}, u32[]{:S(2)}, u32[]{:S(2)}) async-start(bf16[128,4,320]{0,2,1:T(8,128)(2,1)} %bitcast.20), calls=%async_computation.4 | async-start | bytes 655360 | tf_op jit(solution)/shard_map/all_to_all | solution.py:121
  63.0 5.8 %all-to-all-done.4 = bf16[128,4,320]{0,2,1:T(8,128)(2,1)S(1)} async-done(((bf16[128,4,320]{0,2,1:T(8,128)(2,1)}), bf16[128,4,320]{0,2,1:T(8,128)(2,1)S(1)}, u32[]{:S(2)}, u32[]{:S(2)}) %all-to-all-start.4) | async-done | bytes 327712 | tf_op jit(solution)/shard_map/all_to_all | solution.py:121
  69.2 3.6 %fusion.34 = (f32[4,512]{1,0:T(4,128)S(1)}, f32[4,512,512]{1,2,0:T(8,128)}) fusion(pred[512]{0:T(512)(128)(4,1)S(1)} %iota_compare_fusion.1, bf16[512,4,80]{0,2,1:T(8,128)(2,1)S(1)} %reshape.205, bf16[512,4,80]{0,2,1:T(8,128)(2,1)S(1)} %reshape.206), kind=kOutput, calls=%fused_computation.72 | convolution fusion | flops 171966976 | bytes 4858368 | tf_op jit(solution)/shard_map/while/body/eval_jaxpr/sub | solution.py:82
  72.9 2.2 %convolution_convert_fusion = bf16[512,320]{0,1:T(8,128)(2,1)S(1)} fusion(bf16[512,1280]{1,0:T(8,128)(2,1)} %all-gather.2.cloned.1.call-done, bf16[320,1280]{1,0:T(8,128)(2,1)} %param.12), kind=kOutput, calls=%fused_computation.20 | convolution fusion | flops 419594240 | bytes 2457600 | tf_op jit(solution)/shard_map/pd,cd->pc/dot_general | solution.py:127
  75.0 2.9 %fusion.12 = bf16[512,4,80]{0,2,1:T(8,128)(2,1)S(1)} fusion(bf16[512,4,80]{0,2,1:T(8,128)(2,1)S(1)} %bitcast.121, f32[4,512,512]{1,2,0:T(8,128)} %get-tuple-element.51, f32[4,512]{1,0:T(4,128)S(1)} %get-tuple-element.50), kind=kOutput, calls=%fused_computation.21 | convolution fusion | flops 170033152 | bytes 4857856 | tf_op jit(solution)/shard_map/while/body/eval_jaxpr/hbk,bhe->khe/dot_general | solution.py:85
  78.8 4.1 %all-to-all-start.7 = ((bf16[4,128,320]{1,2,0:T(8,128)(2,1)}), bf16[4,128,320]{1,2,0:T(8,128)(2,1)}, u32[]{:S(2)}, u32[]{:S(2)}) async-start(bf16[4,128,320]{1,2,0:T(8,128)(2,1)} %copy.65), calls=%async_computation.7 | async-start | bytes 655360 | tf_op jit(solution)/shard_map/all_to_all | solution.py:153
  83.0 3.1 %multiply_reduce_fusion = (f32[4,512]{1,0:T(4,128)S(1)}, f32[4,512,512]{1,2,0:T(8,128)S(1)}) fusion(f32[4,512,512]{1,2,0:T(8,128)} %get-tuple-element.51, f32[4,512]{1,0:T(4,128)S(1)} %get-tuple-element.50, bf16[512,4,80]{0,2,1:T(8,128)(2,1)S(1)} %bitcast.122, bf16[512,4,80]{0,2,1:T(8,128)(2,1)S(1)} %reshape.209), kind=kOutput, calls=%fused_computation.5 | convolution fusion | flops 170915840 | bytes 9060352 | tf_op jit(solution)/shard_map/while/body/eval_jaxpr/bhe,khe->hbk/dot_general | solution.py:88
  89.1 1.8 %reshape.211 = bf16[4,128,320]{1,0,2:T(4,128)(2,1)} reshape(bf16[512,4,80]{0,2,1:T(8,128)(2,1)} %fusion.16) | data formatting | bytes 655360 | tf_op jit(solution)/shard_map/reshape | solution.py:62
  90.9 1.7 %copy.63 = bf16[4,128,320]{1,2,0:T(8,128)(2,1)} copy(bf16[4,128,320]{1,0,2:T(4,128)(2,1)} %reshape.211) | data formatting | bytes 655360 | tf_op jit(solution)/shard_map/reshape | solution.py:62
  92.6 4.1 %all-to-all-start.6 = ((bf16[4,128,320]{1,2,0:T(8,128)(2,1)}), bf16[4,128,320]{1,2,0:T(8,128)(2,1)}, u32[]{:S(2)}, u32[]{:S(2)}) async-start(bf16[4,128,320]{1,2,0:T(8,128)(2,1)} %copy.63), calls=%async_computation.6 | async-start | bytes 655360 | tf_op jit(solution)/shard_map/all_to_all | solution.py:146
  96.7 2.2 %fusion.15 = bf16[512,4,80]{0,2,1:T(8,128)(2,1)} fusion(bf16[512,4,80]{0,2,1:T(8,128)(2,1)} %copy-done.3, bf16[4,512,512]{1,2,0:T(8,128)(2,1)S(1)} %multiply_convert_fusion), kind=kOutput, calls=%fused_computation.22 | convolution fusion | flops 168099840 | bytes 2752512 | tf_op jit(solution)/shard_map/while/body/eval_jaxpr/hbk,khe->bhe/dot_general | solution.py:92
  100.7 2.8 %all-to-all-done.6 = bf16[4,128,320]{1,2,0:T(8,128)(2,1)} async-done(((bf16[4,128,320]{1,2,0:T(8,128)(2,1)}), bf16[4,128,320]{1,2,0:T(8,128)(2,1)}, u32[]{:S(2)}, u32[]{:S(2)}) %all-to-all-start.6) | async-done | bytes 327712 | tf_op jit(solution)/shard_map/all_to_all | solution.py:146
  103.5 3.5 %all-to-all-start.5 = ((bf16[4,128,320]{1,2,0:T(8,128)(2,1)}), bf16[4,128,320]{1,2,0:T(8,128)(2,1)S(1)}, u32[]{:S(2)}, u32[]{:S(2)}) async-start(bf16[4,128,320]{1,2,0:T(8,128)(2,1)} %copy.61), calls=%async_computation.5 | async-start | bytes 655360 | tf_op jit(solution)/shard_map/all_to_all | solution.py:139
  106.9 42.3 %psum.7 = f32[1280]{0:T(1024)} all-reduce(f32[1280]{0:T(1024)S(1)} %get-tuple-element.46), channel_id=1, replica_groups=mesh['img'=8,'tile'=4] {'img','tile'}, use_global_device_ids=true, to_apply=%region_9.10 | all-reduce | flops 1280 | bytes 10240 | tf_op jit(solution)/shard_map/psum | solution.py:133
  149.2 1.9 %copy.68 = bf16[1,128,1280]{2,1,0:T(8,128)(2,1)} copy(bf16[1,128,1280]{1,2,0:T(8,128)(2,1)} %bitcast.34) | data formatting | bytes 655360
  151.1 1.9 %copy.67 = bf16[1,128,1280]{2,1,0:T(8,128)(2,1)} copy(bf16[1,128,1280]{1,2,0:T(8,128)(2,1)} %bitcast.30) | data formatting | bytes 655360
  (69 shorter events, 18.3 us)
Async XLA Ops:
  7.2 11.2 %copy-start = (bf16[1,128,5120]{2,1,0:T(8,128)(2,1)S(1)}, bf16[1,128,5120]{2,1,0:T(8,128)(2,1)}, u32[]{:S(2)}) copy-start(bf16[1,128,5120]{2,1,0:T(8,128)(2,1)} %param.15) | copy-start | bytes 3932164
  10.3 8.0 %all-to-all-start.2 = ((s32[4,1,16]{2,1,0:T(1,128)}), s32[4,1,16]{2,1,0:T(1,128)S(1)}, u32[]{:S(2)}, u32[]{:S(2)}) async-start(s32[4,1,16]{2,1,0:T(1,128)} %bitcast.12), calls=%async_computation.2 | async-start | bytes 4096 | tf_op jit(solution)/shard_map/all_to_all | solution.py:28
  18.4 5.9 %copy-start.2 = (bf16[1,128,1280]{2,1,0:T(8,128)(2,1)S(1)}, bf16[1,128,1280]{2,1,0:T(8,128)(2,1)}, u32[]{:S(2)}) copy-start(bf16[1,128,1280]{2,1,0:T(8,128)(2,1)} %param.13) | copy-start | bytes 983044
  19.3 15.8 %copy-start.9 = (f32[1280]{0:T(1024)S(1)}, f32[1280]{0:T(1024)}, u32[]{:S(2)}) copy-start(f32[1280]{0:T(1024)} %param.14) | copy-start | bytes 15364
  19.4 17.2 %copy-start.6 = (bf16[1,128,1280]{2,1,0:T(8,128)(2,1)S(1)}, bf16[1,128,1280]{2,1,0:T(8,128)(2,1)}, u32[]{:S(2)}) copy-start(bf16[1,128,1280]{2,1,0:T(8,128)(2,1)} %param.9) | copy-start | bytes 983044
  20.4 20.6 %copy-start.7 = (bf16[1,128,1280]{2,1,0:T(8,128)(2,1)S(1)}, bf16[1,128,1280]{2,1,0:T(8,128)(2,1)}, u32[]{:S(2)}) copy-start(bf16[1,128,1280]{2,1,0:T(8,128)(2,1)} %param.10) | copy-start | bytes 983044
  20.4 13.8 %all-to-all-start.3 = ((bf16[4,16,5120]{2,1,0:T(8,128)(2,1)}), bf16[4,16,5120]{2,1,0:T(8,128)(2,1)S(1)}, u32[]{:S(2)}, u32[]{:S(2)}) async-start(bf16[4,16,5120]{2,1,0:T(8,128)(2,1)} %select_select_fusion), calls=%async_computation.3 | async-start | bytes 1310720 | tf_op jit(solution)/shard_map/all_to_all | solution.py:33
  24.0 48.9 %all-gather.2.cloned.1.call-start = ((), (), s32[]{:S(2)}) async-start(), calls=%async_computation.8 | async-start | bytes 1638400 | tf_op jit(solution)/shard_map/all_gather | solution.py:129
  34.9 17.1 %copy-start.8 = (bf16[1,128,1280]{2,1,0:T(8,128)(2,1)S(1)}, bf16[1,128,1280]{2,1,0:T(8,128)(2,1)}, u32[]{:S(2)}) copy-start(bf16[1,128,1280]{2,1,0:T(8,128)(2,1)} %param.11) | copy-start | bytes 983044
  37.5 11.1 %all-to-all-start = ((bf16[128,4,320]{0,2,1:T(8,128)(2,1)}), bf16[128,4,320]{0,2,1:T(8,128)(2,1)S(1)}, u32[]{:S(2)}, u32[]{:S(2)}) async-start(bf16[128,4,320]{0,2,1:T(8,128)(2,1)} %bitcast.1), calls=%async_computation | async-start | bytes 655360 | tf_op jit(solution)/shard_map/all_to_all | solution.py:115
  48.5 10.1 %all-to-all-start.1 = ((bf16[128,4,320]{0,2,1:T(8,128)(2,1)}), bf16[128,4,320]{0,2,1:T(8,128)(2,1)S(1)}, u32[]{:S(2)}, u32[]{:S(2)}) async-start(bf16[128,4,320]{0,2,1:T(8,128)(2,1)} %bitcast.4), calls=%async_computation.1 | async-start | bytes 655360 | tf_op jit(solution)/shard_map/all_to_all | solution.py:118
  58.7 10.1 %all-to-all-start.4 = ((bf16[128,4,320]{0,2,1:T(8,128)(2,1)}), bf16[128,4,320]{0,2,1:T(8,128)(2,1)S(1)}, u32[]{:S(2)}, u32[]{:S(2)}) async-start(bf16[128,4,320]{0,2,1:T(8,128)(2,1)} %bitcast.20), calls=%async_computation.4 | async-start | bytes 655360 | tf_op jit(solution)/shard_map/all_to_all | solution.py:121
  62.6 10.3 %copy-start.4 = (bf16[512,4,80]{0,2,1:T(8,128)(2,1)}, bf16[512,4,80]{0,2,1:T(8,128)(2,1)S(1)}, u32[]{:S(2)}) copy-start(bf16[512,4,80]{0,2,1:T(8,128)(2,1)S(1)} %reshape.205) | copy-start | bytes 983044
  63.0 9.9 %copy-start.3 = (bf16[512,4,80]{0,2,1:T(8,128)(2,1)}, bf16[512,4,80]{0,2,1:T(8,128)(2,1)S(1)}, u32[]{:S(2)}) copy-start(bf16[512,4,80]{0,2,1:T(8,128)(2,1)S(1)} %reshape.206) | copy-start | bytes 983044
  78.8 13.8 %all-to-all-start.7 = ((bf16[4,128,320]{1,2,0:T(8,128)(2,1)}), bf16[4,128,320]{1,2,0:T(8,128)(2,1)}, u32[]{:S(2)}, u32[]{:S(2)}) async-start(bf16[4,128,320]{1,2,0:T(8,128)(2,1)} %copy.65), calls=%async_computation.7 | async-start | bytes 655360 | tf_op jit(solution)/shard_map/all_to_all | solution.py:153
  83.0 3.5 %copy-start.1 = (f32[4,512,512]{1,2,0:T(8,128)S(1)}, f32[4,512,512]{1,2,0:T(8,128)}, u32[]{:S(2)}) copy-start(f32[4,512,512]{1,2,0:T(8,128)} %get-tuple-element.51) | copy-start | bytes 12582916
  86.4 1.2 copy-start.5
  92.6 10.9 %all-to-all-start.6 = ((bf16[4,128,320]{1,2,0:T(8,128)(2,1)}), bf16[4,128,320]{1,2,0:T(8,128)(2,1)}, u32[]{:S(2)}, u32[]{:S(2)}) async-start(bf16[4,128,320]{1,2,0:T(8,128)(2,1)} %copy.63), calls=%async_computation.6 | async-start | bytes 655360 | tf_op jit(solution)/shard_map/all_to_all | solution.py:146
  103.5 49.5 %all-to-all-start.5 = ((bf16[4,128,320]{1,2,0:T(8,128)(2,1)}), bf16[4,128,320]{1,2,0:T(8,128)(2,1)S(1)}, u32[]{:S(2)}, u32[]{:S(2)}) async-start(bf16[4,128,320]{1,2,0:T(8,128)(2,1)} %copy.61), calls=%async_computation.5 | async-start | bytes 655360 | tf_op jit(solution)/shard_map/all_to_all | solution.py:139
Sparse Core Ops, SparseCore 0:
  36.7 19.3 all-gather.1
where the time goes:
time: 162 us; the launch traced here: 161 us
  blocking collectives  42.3 us (26%)
  waiting for transfers between devices  33.9 us (21%)
  starting transfers between devices  29.9 us (18%)
  local copies, waits for them, and re-layouts  18.5 us (11%)
  matrix products  15.5 us (10%)
  between operations  15 us (9%)
  other arithmetic  5.51 us (3%)
    psum x1, blocking collectives, body(): gain_grad = lax.psum(gain_part, ('img', 'tile'))  42.3 us
    all_to_all x1, waiting for transfers between devices, splice_back(): lax.all_to_all(found_rows, 'tile', split_axis=0, concat_axis=0, tiled=True)  9.75 us
    unnamed x27, local copies, waits for them, and re-layouts  7.72 us
    all_to_all x1, waiting for transfers between devices, body(): lax.all_to_all(to_heads(query[0], tile_count), 'tile', split_axis=1, conc...  6.72 us
    reshape x6, local copies, waits for them, and re-layouts, from_heads(): return result.reshape(tile_count, rows_here, -1)  6.2 us
    all_to_all x1, waiting for transfers between devices, body(): lax.all_to_all(to_heads(values[0], tile_count), 'tile', split_axis=1, con...  5.84 us
    all_to_all x1, waiting for transfers between devices, body(): lax.all_to_all(to_heads(keys[0], tile_count), 'tile', split_axis=1, conca...  5.77 us
    all_to_all x1, starting transfers between devices, splice_back(): lax.all_to_all(requests, 'tile', split_axis=0, concat_axis=0, tiled=True)  4.26 us
  transfers between devices with their start and end apart: 9, of which 6 were waited for; matrix products, arithmetic and copies ran while one was open for 15% of the time, Pallas kernels for 0%

commit v1 on v0

--- a/solution.py
+++ b/solution.py
@@ -1,12 +1,18 @@
+import functools
+
 import jax
 import jax.numpy as jnp
 from jax import lax
+from jax.experimental import pallas as pl
+from jax.experimental.pallas import tpu as pltpu
 from jax.sharding import PartitionSpec as P
 
 HEAD = 80
 
 
 norm_eps = 1e-06
+low = jnp.bfloat16
+full = jnp.float32
 
 
 def splice_back(seq_grad, splice_at, merged_count, width):
@@ -107,20 +113,13 @@
     return (grad_q, (grad_k * factor).astype(jnp.bfloat16), grad_v.astype(jnp.bfloat16))
 
 
-def body(query, keys, values, out_weight, hidden, gain, seq_grad, splice_at, merged_count):
+def general_body(query, keys, values, out_weight, hidden, gain, seq_grad, splice_at, merged_count):
     tile_count = lax.axis_size("tile")
     width = query.shape[-1]
     rows_here = query.shape[1]
     head_q, head_k, head_v = (
-        lax.all_to_all(
-            to_heads(query[0], tile_count), "tile", split_axis=1, concat_axis=0, tiled=True
-        ),
-        lax.all_to_all(
-            to_heads(keys[0], tile_count), "tile", split_axis=1, concat_axis=0, tiled=True
-        ),
-        lax.all_to_all(
-            to_heads(values[0], tile_count), "tile", split_axis=1, concat_axis=0, tiled=True
-        ),
+        lax.all_to_all(to_heads(part[0], tile_count), "tile", split_axis=1, concat_axis=0, tiled=True)
+        for part in (query, keys, values)
     )
     patch_grad = splice_back(seq_grad, splice_at, merged_count, width)
     attn_grad, gain_part = norm_backward(hidden, gain, patch_grad)
@@ -132,38 +131,274 @@
     ).astype(jnp.bfloat16)
     gain_grad = lax.psum(gain_part, ("img", "tile"))
     valid_keys = 4 * merged_count[0]
-    grad_q, grad_k, grad_v = attend(
+    grads = attend(
         head_view(head_q), head_view(head_k), head_view(head_v), head_view(head_g), valid_keys
     )
     back_q, back_k, back_v = (
         lax.all_to_all(
-            from_heads(grad_q, tile_count, rows_here),
-            "tile",
-            split_axis=0,
-            concat_axis=2,
-            tiled=True,
-        ),
-        lax.all_to_all(
-            from_heads(grad_k, tile_count, rows_here),
-            "tile",
-            split_axis=0,
-            concat_axis=2,
-            tiled=True,
-        ),
-        lax.all_to_all(
-            from_heads(grad_v, tile_count, rows_here),
-            "tile",
-            split_axis=0,
-            concat_axis=2,
-            tiled=True,
-        ),
+            from_heads(part, tile_count, rows_here), "tile", split_axis=0, concat_axis=2, tiled=True
+        )
+        for part in grads
     )
     return (back_q, back_k, back_v, gain_grad)
 
 
+NT = (((1,), (1,)), ((), ()))
+NN = (((1,), (0,)), ((), ()))
+TN = (((0,), (0,)), ((), ()))
+
+
+def dot(left, right, form):
+    return lax.dot_general(left, right, form, preferred_element_type=full)
+
+
+def iota(shape, axis):
+    return lax.broadcasted_iota(jnp.int32, shape, axis)
+
+
+def ones_where(condition):
+    return jnp.where(condition, 1.0, 0.0).astype(full)
+
+
+def halves(width):
+    pair = lax.div(lax.axis_index("tile"), 2)
+    half = width // 2
+    mine = pl.multiple_of(pair * half, 128)
+    other = pl.multiple_of((1 - pair) * half, 128)
+    return half, pl.ds(mine, half), pl.ds(other, half)
+
+
+def run(kernel, name, outs, args, scalars=0, scratch=()):
+    smem = pl.BlockSpec(memory_space=pltpu.SMEM)
+    vmem = pl.BlockSpec(memory_space=pltpu.VMEM)
+    return pl.pallas_call(
+        kernel,
+        name=name,
+        out_shape=[jax.ShapeDtypeStruct(shape, kind) for shape, kind in outs],
+        in_specs=[smem] * scalars + [vmem] * (len(args) - scalars),
+        out_specs=[vmem] * len(outs),
+        scratch_shapes=list(scratch),
+        compiler_params=pltpu.CompilerParams(vmem_limit_bytes=48 * 1024 * 1024),
+    )(*args)
+
+
+def pack_kernel(q_ref, k_ref, v_ref, qs_ref, kvs_ref, kvo_ref):
+    half, mine, other = halves(q_ref.shape[1])
+    qs_ref[...] = q_ref[:, other]
+    kvs_ref[:, :half] = k_ref[:, other]
+    kvs_ref[:, half:] = v_ref[:, other]
+    kvo_ref[:, :half] = k_ref[:, mine]
+    kvo_ref[:, half:] = v_ref[:, mine]
+
+
+def earlier(count):
+    return ones_where(iota((count, count), 0) < iota((count, count), 1))
+
+
+def reply_kernel(p0, p1, p2, p3, seq_ref, o0, o1, o2, o3):
+    span, width = seq_ref.shape
+    rows = p0.shape[1]
+    cap = o0.shape[0]
+    base = lax.axis_index("tile") * span
+    before = earlier(rows)
+    picks = []
+    for place in (p0, p1, p2, p3):
+        within = place[...] - base
+        here = ones_where((within >= 0) & (within < span))
+        rank = dot(jnp.broadcast_to(here, (8, rows)), before, NN)[:1]
+        to_slot = ones_where(iota((cap, rows), 0).astype(full) == rank) * here
+        to_place = ones_where(iota((span, rows), 0) == within)
+        picks.append(dot(to_slot.astype(low), to_place.astype(low), NT))
+    pick = jnp.concatenate(picks, axis=0).astype(low)
+    step = width // 4
+    for start in range(0, width, step):
+        found = dot(pick, seq_ref[:, start : start + step], NN).astype(low)
+        for x, out in enumerate((o0, o1, o2, o3)):
+            out[:, start : start + step] = found[x * cap : (x + 1) * cap]
+
+
+def norm_kernel(span, count_ref, place_ref, r0, r1, r2, r3, hidden_ref, gain_ref, attn_ref, part_ref, rows_buf, up_buf):
+    me = lax.axis_index("tile")
+    rows = place_ref.shape[1]
+    cap = r0.shape[0]
+    patches, width = hidden_ref.shape
+    per = patches // rows
+    for x, reply in enumerate((r0, r1, r2, r3)):
+        rows_buf[x * cap : (x + 1) * cap] = reply[...]
+    place = place_ref[...]
+    here = jnp.zeros((8, rows), full)
+    for x in range(4):
+        within = place - jnp.bitwise_xor(me, x) * span
+        inside = ones_where((within >= 0) & (within < span))
+        here = here + ones_where(iota((8, rows), 0) == x) * inside
+    rank = dot(here, earlier(rows), NN)
+    slot = jnp.sum(here * (rank + cap * iota((8, rows), 0).astype(full)), axis=0, keepdims=True)
+    from_slot = ones_where(iota((4 * cap, rows), 0).astype(full) == slot)
+    live = ones_where(iota((1, rows), 1) + me * rows < count_ref[0])
+    total = None
+    for j in range(per):
+        spread = ones_where(iota((patches, rows), 0) == per * iota((patches, rows), 1) + j) * live
+        pick = dot(spread.astype(low), from_slot.astype(low), NT).astype(low)
+        part = dot(pick, rows_buf[:, j * width : (j + 1) * width], NN)
+        total = part if total is None else total + part
+    up_buf[...] = total
+    gain = gain_ref[...]
+    step = 16
+    kept = jnp.zeros((step, width), full)
+    for start in range(0, patches, step):
+        held = hidden_ref[start : start + step].astype(full)
+        inverse = lax.rsqrt(jnp.mean(held * held, axis=-1, keepdims=True) + norm_eps)
+        normed = held * inverse
+        upstream = up_buf[start : start + step]
+        kept = kept + upstream * normed
+        scaled = gain * upstream
+        mean = jnp.mean(scaled * normed, axis=-1, keepdims=True)
+        attn_ref[start : start + step] = (inverse * (scaled - normed * mean)).astype(low)
+    part_ref[...] = jnp.sum(kept, axis=0, keepdims=True)
+
+
+def attend_kernel(
+    count_ref, q_ref, q2_ref, kv0, kv1, kv2, kv3, a0, a2, w0, w1,
+    dq0_ref, dq2_ref, send_ref, keep_ref,
+    q_buf, k_buf, v_buf, g_buf, w_buf, bias_buf, dqt_buf, dk_buf, dv_buf,
+):
+    me = lax.axis_index("tile")
+    core = lax.rem(me, 2)
+    rows, width = q_ref.shape
+    half, mine, other = halves(width)
+    channels = w0.shape[0]
+    w_buf[pl.ds(pl.multiple_of(core * channels, channels), channels)] = w0[...]
+    w_buf[pl.ds(pl.multiple_of((1 - core) * channels, channels), channels)] = w1[...]
+    q_buf[:rows] = q_ref[:, mine]
+    q_buf[rows:] = q2_ref[...]
+    valid = count_ref[0] * 4
+    for x, part in enumerate((kv0, kv1, kv2, kv3)):
+        block = slice(x * rows, (x + 1) * rows)
+        k_buf[block] = part[:, :half]
+        v_buf[block] = part[:, half:]
+        index = jnp.bitwise_xor(me, x) * rows + iota((rows, 128), 0)
+        bias_buf[block] = jnp.where(index < valid, 0.0, -1e30).astype(full)
+    g_buf[:rows] = dot(a0[...], w_buf[...], NT).astype(low)
+    g_buf[rows:] = dot(a2[...], w_buf[...], NT).astype(low)
+    factor = HEAD ** (-0.5)
+    for start in range(0, half, HEAD):
+        columns = slice(start, start + HEAD)
+        q = q_buf[:, columns]
+        k = k_buf[:, columns]
+        v = v_buf[:, columns]
+        g = g_buf[:, columns]
+        scores = dot(k, q, NT) * factor + bias_buf[:, :1]
+        expons = jnp.exp(scores - jnp.max(scores, axis=0, keepdims=True))
+        probs = expons * (1.0 / jnp.sum(expons, axis=0, keepdims=True))
+        dv_buf[:, columns] = dot(probs.astype(low), g, NN)
+        dprobs = dot(v, g, NT)
+        spread = jnp.sum(probs * dprobs, axis=0, keepdims=True)
+        dscores = (probs * (dprobs - spread)).astype(low)
+        dk_buf[:, columns] = dot(dscores, q, NN) * factor
+        dqt_buf[columns] = dot(k, dscores, TN) * factor
+    dq = jnp.transpose(dqt_buf[...])
+    dq0_ref[...] = dq[:rows].astype(low)
+    dq2_ref[...] = dq[rows:].astype(low)
+    for x in range(2):
+        keep = slice(2 * x * rows, (2 * x + 1) * rows)
+        send = slice((2 * x + 1) * rows, (2 * x + 2) * rows)
+        out = slice(x * rows, (x + 1) * rows)
+        keep_ref[out, :half] = dk_buf[keep]
+        keep_ref[out, half:] = dv_buf[keep]
+        send_ref[out, :half] = dk_buf[send]
+        send_ref[out, half:] = dv_buf[send]
+
+
+def add_kernel(keep_ref, came_ref, own_ref, back_ref):
+    rows = own_ref.shape[0]
+    own_ref[...] = (keep_ref[:rows] + came_ref[:rows]).astype(low)
+    back_ref[...] = (keep_ref[rows:] + came_ref[rows:]).astype(low)
+
+
+def join_kernel(dq0, dqr, own, back, q_out, k_out, v_out):
+    half, mine, other = halves(q_out.shape[1])
+    q_out[:, mine] = dq0[...]
+    q_out[:, other] = dqr[...]
+    k_out[:, mine] = own[:, :half]
+    k_out[:, other] = back[:, :half]
+    v_out[:, mine] = own[:, half:]
+    v_out[:, other] = back[:, half:]
+
+
+def swap(value, x, axis="tile"):
+    return lax.ppermute(value, axis, [(i, i ^ x) for i in range(lax.axis_size(axis))])
+
+
+def sum_everywhere(part):
+    for axis in ("tile", "img"):
+        x = 1
+        while x < lax.axis_size(axis):
+            part = part + swap(part, x, axis)
+            x *= 2
+    return part
+
+
+def pairs_body(query, keys, values, out_weight, hidden, gain, seq_grad, splice_at, merged_count):
+    rows, width = query.shape[1:]
+    half = width // 2
+    asked = splice_at.shape[1]
+    span, seq_width = seq_grad.shape[1:]
+    cap = asked // 2
+    vmem = pltpu.VMEM
+
+    place = [splice_at] + [swap(splice_at, x) for x in (1, 2, 3)]
+    q_send, kv_send, kv0 = run(
+        pack_kernel, "pack",
+        [((rows, half), low), ((rows, width), low), ((rows, width), low)],
+        (query[0], keys[0], values[0]),
+    )
+    kv2 = swap(kv_send, 2)
+    q2 = swap(q_send, 2)
+    kv1 = swap(kv0, 1)
+    kv3 = swap(kv2, 1)
+    weight1 = swap(out_weight, 1)
+
+    found = run(reply_kernel, "reply", [((cap, seq_width), low)] * 4, (*place, seq_grad[0]))
+    replies = [found[0]] + [swap(found[x], x) for x in (1, 2, 3)]
+    attn0, gain_part = run(
+        functools.partial(norm_kernel, span), "norm",
+        [((rows, width), low), ((1, width), full)],
+        (merged_count, splice_at, *replies, hidden[0], gain[None]),
+        scalars=1,
+        scratch=[vmem((4 * cap, seq_width), low), vmem((rows, width), full)],
+    )
+    attn2 = swap(attn0, 2)
+    gain_grad = sum_everywhere(gain_part)[0]
+
+    dq0, dq_send, send, keep = run(
+        attend_kernel, "attend",
+        [((rows, half), low), ((rows, half), low), ((2 * rows, width), full), ((2 * rows, width), full)],
+        (merged_count, query[0], q2, kv0, kv1, kv2, kv3, attn0, attn2, out_weight, weight1),
+        scalars=1,
+        scratch=[
+            vmem((2 * rows, half), low), vmem((4 * rows, half), low), vmem((4 * rows, half), low),
+            vmem((2 * rows, half), low), vmem((half, width), low), vmem((4 * rows, 128), full),
+            vmem((half, 2 * rows), full), vmem((4 * rows, half), full), vmem((4 * rows, half), full),
+        ],
+    )
+    came = swap(send, 1)
+    dq_back = swap(dq_send, 2)
+    own, back_send = run(
+        add_kernel, "add", [((rows, width), low)] * 2, (keep, came)
+    )
+    back = swap(back_send, 2)
+    grads = run(join_kernel, "join", [((rows, width), low)] * 3, (dq0, dq_back, own, back))
+    return (*(part[None] for part in grads), gain_grad)
+
+
+def power_of_two(count):
+    return count & (count - 1) == 0
+
+
 def solution(mesh):
+    paired = mesh.shape["tile"] == 4 and power_of_two(mesh.shape["img"])
     return jax.shard_map(
-        body,
+        pairs_body if paired else general_body,
         mesh=mesh,
         in_specs=(
             P("img", "tile", None),

time: 162 us -> 82.7 us (0.51)
  blocking collectives: 42.3 us -> 0 us
  matrix products: 15.5 us -> 0 us
  between operations: 15 us -> 1.4 us
  local copies, waits for them, and re-layouts: 18.5 us -> 6.23 us
  Pallas kernels: 0 us -> 11.6 us
  starting transfers between devices: 29.9 us -> 20 us
  waiting for transfers between devices: 33.9 us -> 42.5 us
  other arithmetic: 5.51 us -> 0.65 us
    ppermute x0 -> x20, waiting for transfers between devices: none -> 42.5 us  [swap(): lax.ppermute(value, axis, [(i, i ^ x) for i in range(lax.axis_size(axis))])]
    psum x1 -> x0, blocking collectives: 42.3 us -> none  [body(): gain_grad = lax.psum(gain_part, ('img', 'tile'))]
    all_to_all x8 -> x0, waiting for transfers between devices: 33.9 us -> none  [the longest x1 9.75 us: splice_back(): lax.all_to_all(found_rows, 'tile', split_axis=0, concat_axis=0, tiled=True)]
    all_to_all x8 -> x0, starting transfers between devices: 29.9 us -> none  [the longest x1 4.26 us: splice_back(): lax.all_to_all(requests, 'tile', split_axis=0, concat_axis=0, tiled=True)]
    ppermute x0 -> x20, starting transfers between devices: none -> 20 us  [swap(): lax.ppermute(value, axis, [(i, i ^ x) for i in range(lax.axis_size(axis))])]
    dot_general x5 -> x0, matrix products: 11.9 us -> none  [the longest x1 3.11 us: one_block(): jnp.einsum('bhe,khe->hbk', grads_block, head_v, preferred_element_type=jn...]
    pallas_call x0 -> x6, Pallas kernels: none -> 11.6 us  [run(): pl.pallas_call(kernel, name=name, out_shape=[jax.ShapeDtypeStruct(shape,...]
    reshape x9 -> x0, local copies, waits for them, and re-layouts: 6.58 us -> none  [the longest x6 6.2 us: from_heads(): return result.reshape(tile_count, rows_here, -1)]
  transfers between devices with their start and end apart: 9 -> 20, of which waited for: 6 -> 10; matrix products, arithmetic and copies ran while one was open for 15% -> 1% of each run, Pallas kernels for 0% -> 2%
where the time goes in v1:
time: 82.7 us; the launch traced here: 82.4 us
  waiting for transfers between devices  42.5 us (51%)
  starting transfers between devices  20 us (24%)
  Pallas kernels  11.6 us (14%)
  local copies, waits for them, and re-layouts  6.23 us (8%)
  between operations  1.4 us (2%)
    ppermute x20, waiting for transfers between devices, swap(): lax.ppermute(value, axis, [(i, i ^ x) for i in range(lax.axis_size(axis))])  42.5 us
    ppermute x20, starting transfers between devices, swap(): lax.ppermute(value, axis, [(i, i ^ x) for i in range(lax.axis_size(axis))])  20 us
    pallas_call x6, Pallas kernels, run(): pl.pallas_call(kernel, name=name, out_shape=[jax.ShapeDtypeStruct(shape,...  11.6 us
    unnamed x20, local copies, waits for them, and re-layouts  6.22 us
  transfers between devices with their start and end apart: 20, of which 10 were waited for; matrix products, arithmetic and copies ran while one was open for 1% of the time, Pallas kernels for 2%

profile of v1, /device:TPU:0, one launch (start us, length us, event | category | flops | bytes accessed | tf_op | source)
XLA Modules:
  0.0 82.4 jit_solution(13004059223167889463)
XLA Ops:
  4.2 2.6 %collective-permute-start.2 = (bf16[128,1280]{1,0:T(8,128)(2,1)S(1)}, bf16[128,1280]{1,0:T(8,128)(2,1)S(1)}, u32[]{:S(2)}, u32[]{:S(2)}) collective-permute-start(bf16[128,1280]{1,0:T(8,128)(2,1)S(1)} %get-tuple-element.24), channel_id=1, source_target_pairs={{0,2},{1,3},{2,0},{3,1},{4,6},{5,7},{6,4},{7,5},{8,10},{9,11},{10,... | collective-permute-start | bytes 983048 | tf_op jit(solution)/shard_map/ppermute | solution.py:329
  7.4 1.3 %collective-permute-start.6 = (s32[1,32]{1,0:T(1,128)}, s32[1,32]{1,0:T(1,128)S(1)}, u32[]{:S(2)}, u32[]{:S(2)}) collective-permute-start(s32[1,32]{1,0:T(1,128)} %place_ref.1), channel_id=1, source_target_pairs={{0,3},{1,2},{2,1},{3,0},{4,7},{5,6},{6,5},{7,4},{8,11},{9,10},{10,... | collective-permute-start | bytes 392 | tf_op jit(solution)/shard_map/ppermute | solution.py:329
  8.6 6.6 %collective-permute-done.5.p2 = s32[1,32]{1,0:T(1,128)S(1)} collective-permute-done((s32[1,32]{1,0:T(1,128)}, s32[1,32]{1,0:T(1,128)S(1)}, u32[]{:S(2)}, u32[]{:S(2)}) %collective-permute-start.5) | collective-permute-done | bytes 160 | tf_op jit(solution)/shard_map/ppermute | solution.py:329
  15.3 1.3 %copy-done.2 = bf16[1,128,5120]{2,1,0:T(8,128)(2,1)S(1)} copy-done((bf16[1,128,5120]{2,1,0:T(8,128)(2,1)S(1)}, bf16[1,128,5120]{2,1,0:T(8,128)(2,1)}, u32[]{:S(2)}) %copy-start.2) | copy-done | bytes 1310744
  18.0 1.8 %collective-permute-start.8 = (bf16[16,5120]{1,0:T(8,128)(2,1)S(1)}, bf16[16,5120]{1,0:T(8,128)(2,1)S(1)}, u32[]{:S(2)}, u32[]{:S(2)}) collective-permute-start(bf16[16,5120]{1,0:T(8,128)(2,1)S(1)} %get-tuple-element.27), channel_id=1, source_target_pairs={{0,2},{1,3},{2,0},{3,1},{4,6},{5,7},{6,4},{7,5},{8,10},{9,11},{10,... | collective-permute-start | bytes 491528 | tf_op jit(solution)/shard_map/ppermute | solution.py:329
  20.9 4.2 %collective-permute-done.8.r2 = bf16[16,5120]{1,0:T(8,128)(2,1)S(1)} collective-permute-done((bf16[16,5120]{1,0:T(8,128)(2,1)S(1)}, bf16[16,5120]{1,0:T(8,128)(2,1)S(1)}, u32[]{:S(2)}, u32[]{:S(2)}) %collective-permute-start.8) | collective-permute-done | bytes 163872 | tf_op jit(solution)/shard_map/ppermute | solution.py:329
  25.1 2.4 %collective-permute-done.9.r3 = bf16[16,5120]{1,0:T(8,128)(2,1)S(1)} collective-permute-done((bf16[16,5120]{1,0:T(8,128)(2,1)S(1)}, bf16[16,5120]{1,0:T(8,128)(2,1)S(1)}, u32[]{:S(2)}, u32[]{:S(2)}) %collective-permute-start.9) | collective-permute-done | bytes 163872 | tf_op jit(solution)/shard_map/ppermute | solution.py:329
  27.5 1.2 %norm.1 = (bf16[128,1280]{1,0:T(8,128)(2,1)S(1)}, f32[1,1280]{1,0:T(1,128)S(1)}) custom-call(s32[1]{0:T(128)S(6)} %copy.13.count_ref, s32[1,32]{1,0:T(1,128)S(1)} %copy-done.8, bf16[16,5120]{1,0:T(8,128)(2,1)S(1)} %get-tuple-element.25.r0, bf16[16,5120]{1,0:T(8,128)(2,1)S(1)} %collective-permute-done.7.r1, bf16[16,5120]{1,0:T(8,128)(2,1)S(1)} %collective-permute-done.8.r2, ...), custom_call_target="tpu_custom_call" | custom-call | tf_op jit(solution)/shard_map/norm/pallas_call | solution.py:174
  28.7 1.8 %collective-permute-start.10 = (bf16[128,1280]{1,0:T(8,128)(2,1)S(1)}, bf16[128,1280]{1,0:T(8,128)(2,1)S(1)}, u32[]{:S(2)}, u32[]{:S(2)}) collective-permute-start(bf16[128,1280]{1,0:T(8,128)(2,1)S(1)} %get-tuple-element.29.a0), channel_id=1, source_target_pairs={{0,2},{1,3},{2,0},{3,1},{4,6},{5,7},{6,4},{7,5},{8,10},{9,11},{10,... | collective-permute-start | bytes 983048 | tf_op jit(solution)/shard_map/ppermute | solution.py:329
  31.0 11.3 %collective-permute-done.q2_ref = bf16[128,640]{1,0:T(8,128)(2,1)S(1)} collective-permute-done((bf16[128,640]{1,0:T(8,128)(2,1)S(1)}, bf16[128,640]{1,0:T(8,128)(2,1)S(1)}, u32[]{:S(2)}, u32[]{:S(2)}) %collective-permute-start) | collective-permute-done | bytes 163872 | tf_op jit(solution)/shard_map/ppermute | solution.py:329
  42.4 8.5 %attend.1 = (bf16[128,640]{1,0:T(8,128)(2,1)S(1)}, bf16[128,640]{1,0:T(8,128)(2,1)S(1)}, f32[256,1280]{1,0:T(8,128)S(1)}, f32[256,1280]{1,0:T(8,128)}) custom-call(s32[1]{0:T(128)S(6)} %copy.13.count_ref, bf16[128,1280]{1,0:T(8,128)(2,1)S(1)} %bitcast.9, bf16[128,640]{1,0:T(8,128)(2,1)S(1)} %collective-permute-done.q2_ref, ...), custom_call_target="tpu_custom_call" | custom-call | tf_op jit(solution)/shard_map/attend/pallas_call | solution.py:174
  50.9 3.0 %collective-permute-done.13.came_ref = f32[256,1280]{1,0:T(8,128)S(1)} collective-permute-done((f32[256,1280]{1,0:T(8,128)S(1)}, f32[256,1280]{1,0:T(8,128)S(1)}, u32[]{:S(2)}, u32[]{:S(2)}) %collective-permute-start.13) | collective-permute-done | bytes 1310752 | tf_op jit(solution)/shard_map/ppermute | solution.py:329
  53.9 1.3 %copy-done.3 = f32[256,1280]{1,0:T(8,128)S(1)} copy-done((f32[256,1280]{1,0:T(8,128)S(1)}, f32[256,1280]{1,0:T(8,128)}, u32[]{:S(2)}) %copy-start.3) | copy-done | bytes 1310744
  55.4 1.8 %collective-permute-start.14 = (bf16[128,1280]{1,0:T(8,128)(2,1)S(1)}, bf16[128,1280]{1,0:T(8,128)(2,1)S(1)}, u32[]{:S(2)}, u32[]{:S(2)}) collective-permute-start(bf16[128,1280]{1,0:T(8,128)(2,1)S(1)} %get-tuple-element.35), channel_id=1, source_target_pairs={{0,2},{1,3},{2,0},{3,1},{4,6},{5,7},{6,4},{7,5},{8,10},{9,11},{10,... | collective-permute-start | bytes 983048 | tf_op jit(solution)/shard_map/ppermute | solution.py:329
  57.4 1.2 %collective-permute-done.15 = f32[1,1280]{1,0:T(1,128)S(1)} collective-permute-done((f32[1,1280]{1,0:T(1,128)S(1)}, f32[1,1280]{1,0:T(1,128)S(1)}, u32[]{:S(2)}, u32[]{:S(2)}) %collective-permute-start.15) | collective-permute-done | bytes 5152 | tf_op jit(solution)/shard_map/ppermute | solution.py:329
  58.6 1.8 %collective-permute-start.16 = (f32[1,1280]{1,0:T(1,128)S(1)}, f32[1,1280]{1,0:T(1,128)S(1)}, u32[]{:S(2)}, u32[]{:S(2)}) collective-permute-start(f32[1,1280]{1,0:T(1,128)S(1)} %add.16), channel_id=1, source_target_pairs={{0,2},{1,3},{2,0},{3,1},{4,6},{5,7},{6,4},{7,5},{8,10},{9,11},{10,... | collective-permute-start | bytes 15368 | tf_op jit(solution)/shard_map/ppermute | solution.py:329
  60.4 8.4 %collective-permute-done.16 = f32[1,1280]{1,0:T(1,128)S(1)} collective-permute-done((f32[1,1280]{1,0:T(1,128)S(1)}, f32[1,1280]{1,0:T(1,128)S(1)}, u32[]{:S(2)}, u32[]{:S(2)}) %collective-permute-start.16) | collective-permute-done | bytes 5152 | tf_op jit(solution)/shard_map/ppermute | solution.py:329
  68.8 1.8 %collective-permute-start.17 = (f32[1,1280]{1,0:T(1,128)S(1)}, f32[1,1280]{1,0:T(1,128)S(1)}, u32[]{:S(2)}, u32[]{:S(2)}) collective-permute-start(f32[1,1280]{1,0:T(1,128)S(1)} %add.17), channel_id=1, source_target_pairs={{0,4},{4,0},{8,12},{12,8},{16,20},{20,16},{24,28},{28,24},{1,5},{5... | collective-permute-start | bytes 15368 | tf_op jit(solution)/shard_map/ppermute | solution.py:329
  70.6 1.9 %collective-permute-done.17 = f32[1,1280]{1,0:T(1,128)S(1)} collective-permute-done((f32[1,1280]{1,0:T(1,128)S(1)}, f32[1,1280]{1,0:T(1,128)S(1)}, u32[]{:S(2)}, u32[]{:S(2)}) %collective-permute-start.17) | collective-permute-done | bytes 5152 | tf_op jit(solution)/shard_map/ppermute | solution.py:329
  72.5 1.9 %collective-permute-start.18 = (f32[1,1280]{1,0:T(1,128)S(1)}, f32[1,1280]{1,0:T(1,128)S(1)}, u32[]{:S(2)}, u32[]{:S(2)}) collective-permute-start(f32[1,1280]{1,0:T(1,128)S(1)} %add.18), channel_id=1, source_target_pairs={{0,8},{4,12},{8,0},{12,4},{16,24},{20,28},{24,16},{28,20},{1,9},{5... | collective-permute-start | bytes 15368 | tf_op jit(solution)/shard_map/ppermute | solution.py:329
  74.3 1.8 %collective-permute-done.18 = f32[1,1280]{1,0:T(1,128)S(1)} collective-permute-done((f32[1,1280]{1,0:T(1,128)S(1)}, f32[1,1280]{1,0:T(1,128)S(1)}, u32[]{:S(2)}, u32[]{:S(2)}) %collective-permute-start.18) | collective-permute-done | bytes 5152 | tf_op jit(solution)/shard_map/ppermute | solution.py:329
  76.2 2.9 %collective-permute-start.19 = (f32[1,1280]{1,0:T(1,128)S(1)}, f32[1,1280]{1,0:T(1,128)S(1)}, u32[]{:S(2)}, u32[]{:S(2)}) collective-permute-start(f32[1,1280]{1,0:T(1,128)S(1)} %add.19), channel_id=1, source_target_pairs={{0,16},{4,20},{8,24},{12,28},{16,0},{20,4},{24,8},{28,12},{1,17},{... | collective-permute-start | bytes 15368 | tf_op jit(solution)/shard_map/ppermute | solution.py:329
  79.0 1.7 %collective-permute-done.19 = f32[1,1280]{1,0:T(1,128)S(1)} collective-permute-done((f32[1,1280]{1,0:T(1,128)S(1)}, f32[1,1280]{1,0:T(1,128)S(1)}, u32[]{:S(2)}, u32[]{:S(2)}) %collective-permute-start.19) | collective-permute-done | bytes 5152 | tf_op jit(solution)/shard_map/ppermute | solution.py:329
  81.4 1.0 %join.1 = (bf16[128,1280]{1,0:T(8,128)(2,1)}, bf16[128,1280]{1,0:T(8,128)(2,1)}, bf16[128,1280]{1,0:T(8,128)(2,1)}) custom-call(bf16[128,640]{1,0:T(8,128)(2,1)S(1)} %get-tuple-element.30.dq0, bf16[128,640]{1,0:T(8,128)(2,1)S(1)} %collective-permute-done.12.dqr, bf16[128,1280]{1,0:T(8,128)(2,1)S(1)} %get-tuple-element.34.own, ...), custom_call_target="tpu_custom_call" | custom-call | tf_op jit(solution)/shard_map/join/pallas_call | solution.py:174
  (48 shorter events, 7.5 us)
Async XLA Ops:
  0.6 41.7 %collective-permute-start.11 = (bf16[320,1280]{1,0:T(8,128)(2,1)}, bf16[320,1280]{1,0:T(8,128)(2,1)S(1)}, u32[]{:S(2)}, u32[]{:S(2)}) collective-permute-start(bf16[320,1280]{1,0:T(8,128)(2,1)} %w0.1), channel_id=1, source_target_pairs={{0,1},{1,0},{2,3},{3,2},{4,5},{5,4},{6,7},{7,6},{8,9},{9,8},{10,11... | collective-permute-start | bytes 2457608 | tf_op jit(solution)/shard_map/ppermute | solution.py:329
  4.1 16.4 %copy-start.9 = (f32[1280]{0:T(1024)S(1)}, f32[1280]{0:T(1024)}, u32[]{:S(2)}) copy-start(f32[1280]{0:T(1024)} %param.14) | copy-start | bytes 15364
  4.1 38.2 %copy-start.4 = (bf16[320,1280]{1,0:T(8,128)(2,1)S(1)}, bf16[320,1280]{1,0:T(8,128)(2,1)}, u32[]{:S(2)}) copy-start(bf16[320,1280]{1,0:T(8,128)(2,1)} %w0.1) | copy-start | bytes 2457604
  4.2 38.2 %copy-start.1 = (bf16[1,128,1280]{2,1,0:T(8,128)(2,1)S(1)}, bf16[1,128,1280]{2,1,0:T(8,128)(2,1)}, u32[]{:S(2)}) copy-start(bf16[1,128,1280]{2,1,0:T(8,128)(2,1)} %param.9) | copy-start | bytes 983044
  4.2 26.4 %collective-permute-start.2 = (bf16[128,1280]{1,0:T(8,128)(2,1)S(1)}, bf16[128,1280]{1,0:T(8,128)(2,1)S(1)}, u32[]{:S(2)}, u32[]{:S(2)}) collective-permute-start(bf16[128,1280]{1,0:T(8,128)(2,1)S(1)} %get-tuple-element.24), channel_id=1, source_target_pairs={{0,2},{1,3},{2,0},{3,1},{4,6},{5,7},{6,4},{7,5},{8,10},{9,11},{10,... | collective-permute-start | bytes 983048 | tf_op jit(solution)/shard_map/ppermute | solution.py:329
  6.8 1.9 %collective-permute-start.4 = (s32[1,32]{1,0:T(1,128)}, s32[1,32]{1,0:T(1,128)S(1)}, u32[]{:S(2)}, u32[]{:S(2)}) collective-permute-start(s32[1,32]{1,0:T(1,128)} %place_ref.1), channel_id=1, source_target_pairs={{0,1},{1,0},{2,3},{3,2},{4,5},{5,4},{6,7},{7,6},{8,9},{9,8},{10,11... | collective-permute-start | bytes 392 | tf_op jit(solution)/shard_map/ppermute | solution.py:329
  7.0 8.3 %collective-permute-start.5 = (s32[1,32]{1,0:T(1,128)}, s32[1,32]{1,0:T(1,128)S(1)}, u32[]{:S(2)}, u32[]{:S(2)}) collective-permute-start(s32[1,32]{1,0:T(1,128)} %place_ref.1), channel_id=1, source_target_pairs={{0,2},{1,3},{2,0},{3,1},{4,6},{5,7},{6,4},{7,5},{8,10},{9,11},{10,... | collective-permute-start | bytes 392 | tf_op jit(solution)/shard_map/ppermute | solution.py:329
  7.4 7.9 %collective-permute-start.6 = (s32[1,32]{1,0:T(1,128)}, s32[1,32]{1,0:T(1,128)S(1)}, u32[]{:S(2)}, u32[]{:S(2)}) collective-permute-start(s32[1,32]{1,0:T(1,128)} %place_ref.1), channel_id=1, source_target_pairs={{0,3},{1,2},{2,1},{3,0},{4,7},{5,6},{6,5},{7,4},{8,11},{9,10},{10,... | collective-permute-start | bytes 392 | tf_op jit(solution)/shard_map/ppermute | solution.py:329
  17.2 10.3 %copy-start.7 = (bf16[1,128,1280]{2,1,0:T(8,128)(2,1)S(1)}, bf16[1,128,1280]{2,1,0:T(8,128)(2,1)}, u32[]{:S(2)}) copy-start(bf16[1,128,1280]{2,1,0:T(8,128)(2,1)} %param.13) | copy-start | bytes 983044
  17.9 2.6 %collective-permute-start.7 = (bf16[16,5120]{1,0:T(8,128)(2,1)S(1)}, bf16[16,5120]{1,0:T(8,128)(2,1)S(1)}, u32[]{:S(2)}, u32[]{:S(2)}) collective-permute-start(bf16[16,5120]{1,0:T(8,128)(2,1)S(1)} %get-tuple-element.26), channel_id=1, source_target_pairs={{0,1},{1,0},{2,3},{3,2},{4,5},{5,4},{6,7},{7,6},{8,9},{9,8},{10,11... | collective-permute-start | bytes 491528 | tf_op jit(solution)/shard_map/ppermute | solution.py:329
  18.0 7.1 %collective-permute-start.8 = (bf16[16,5120]{1,0:T(8,128)(2,1)S(1)}, bf16[16,5120]{1,0:T(8,128)(2,1)S(1)}, u32[]{:S(2)}, u32[]{:S(2)}) collective-permute-start(bf16[16,5120]{1,0:T(8,128)(2,1)S(1)} %get-tuple-element.27), channel_id=1, source_target_pairs={{0,2},{1,3},{2,0},{3,1},{4,6},{5,7},{6,4},{7,5},{8,10},{9,11},{10,... | collective-permute-start | bytes 491528 | tf_op jit(solution)/shard_map/ppermute | solution.py:329
  19.8 7.8 %collective-permute-start.9 = (bf16[16,5120]{1,0:T(8,128)(2,1)S(1)}, bf16[16,5120]{1,0:T(8,128)(2,1)S(1)}, u32[]{:S(2)}, u32[]{:S(2)}) collective-permute-start(bf16[16,5120]{1,0:T(8,128)(2,1)S(1)} %get-tuple-element.28), channel_id=1, source_target_pairs={{0,3},{1,2},{2,1},{3,0},{4,7},{5,6},{6,5},{7,4},{8,11},{9,10},{10,... | collective-permute-start | bytes 491528 | tf_op jit(solution)/shard_map/ppermute | solution.py:329
  20.5 21.8 %collective-permute-start.1 = (bf16[128,1280]{1,0:T(8,128)(2,1)S(1)}, bf16[128,1280]{1,0:T(8,128)(2,1)S(1)}, u32[]{:S(2)}, u32[]{:S(2)}) collective-permute-start(bf16[128,1280]{1,0:T(8,128)(2,1)S(1)} %get-tuple-element.23.kv0), channel_id=1, source_target_pairs={{0,1},{1,0},{2,3},{3,2},{4,5},{5,4},{6,7},{7,6},{8,9},{9,8},{10,11... | collective-permute-start | bytes 983048 | tf_op jit(solution)/shard_map/ppermute | solution.py:329
  28.7 13.6 %collective-permute-start.10 = (bf16[128,1280]{1,0:T(8,128)(2,1)S(1)}, bf16[128,1280]{1,0:T(8,128)(2,1)S(1)}, u32[]{:S(2)}, u32[]{:S(2)}) collective-permute-start(bf16[128,1280]{1,0:T(8,128)(2,1)S(1)} %get-tuple-element.29.a0), channel_id=1, source_target_pairs={{0,2},{1,3},{2,0},{3,1},{4,6},{5,7},{6,4},{7,5},{8,10},{9,11},{10,... | collective-permute-start | bytes 983048 | tf_op jit(solution)/shard_map/ppermute | solution.py:329
  30.6 11.8 %collective-permute-start.3 = (bf16[128,1280]{1,0:T(8,128)(2,1)S(1)}, bf16[128,1280]{1,0:T(8,128)(2,1)S(1)}, u32[]{:S(2)}, u32[]{:S(2)}) collective-permute-start(bf16[128,1280]{1,0:T(8,128)(2,1)S(1)} %collective-permute-done.2.kv2), channel_id=1, source_target_pairs={{0,1},{1,0},{2,3},{3,2},{4,5},{5,4},{6,7},{7,6},{8,9},{9,8},{10,11... | collective-permute-start | bytes 983048 | tf_op jit(solution)/shard_map/ppermute | solution.py:329
  30.6 11.7 %collective-permute-start = (bf16[128,640]{1,0:T(8,128)(2,1)S(1)}, bf16[128,640]{1,0:T(8,128)(2,1)S(1)}, u32[]{:S(2)}, u32[]{:S(2)}) collective-permute-start(bf16[128,640]{1,0:T(8,128)(2,1)S(1)} %get-tuple-element.22), channel_id=1, source_target_pairs={{0,2},{1,3},{2,0},{3,1},{4,6},{5,7},{6,4},{7,5},{8,10},{9,11},{10,... | collective-permute-start | bytes 491528 | tf_op jit(solution)/shard_map/ppermute | solution.py:329
  50.9 3.0 %collective-permute-start.13 = (f32[256,1280]{1,0:T(8,128)S(1)}, f32[256,1280]{1,0:T(8,128)S(1)}, u32[]{:S(2)}, u32[]{:S(2)}) collective-permute-start(f32[256,1280]{1,0:T(8,128)S(1)} %get-tuple-element.33), channel_id=1, source_target_pairs={{0,1},{1,0},{2,3},{3,2},{4,5},{5,4},{6,7},{7,6},{8,9},{9,8},{10,11... | collective-permute-start | bytes 3932168 | tf_op jit(solution)/shard_map/ppermute | solution.py:329
  55.4 26.0 %collective-permute-start.14 = (bf16[128,1280]{1,0:T(8,128)(2,1)S(1)}, bf16[128,1280]{1,0:T(8,128)(2,1)S(1)}, u32[]{:S(2)}, u32[]{:S(2)}) collective-permute-start(bf16[128,1280]{1,0:T(8,128)(2,1)S(1)} %get-tuple-element.35), channel_id=1, source_target_pairs={{0,2},{1,3},{2,0},{3,1},{4,6},{5,7},{6,4},{7,5},{8,10},{9,11},{10,... | collective-permute-start | bytes 983048 | tf_op jit(solution)/shard_map/ppermute | solution.py:329
  57.2 24.2 %collective-permute-start.12 = (bf16[128,640]{1,0:T(8,128)(2,1)S(1)}, bf16[128,640]{1,0:T(8,128)(2,1)S(1)}, u32[]{:S(2)}, u32[]{:S(2)}) collective-permute-start(bf16[128,640]{1,0:T(8,128)(2,1)S(1)} %get-tuple-element.31), channel_id=1, source_target_pairs={{0,2},{1,3},{2,0},{3,1},{4,6},{5,7},{6,4},{7,5},{8,10},{9,11},{10,... | collective-permute-start | bytes 491528 | tf_op jit(solution)/shard_map/ppermute | solution.py:329
  57.4 1.2 %collective-permute-start.15 = (f32[1,1280]{1,0:T(1,128)S(1)}, f32[1,1280]{1,0:T(1,128)S(1)}, u32[]{:S(2)}, u32[]{:S(2)}) collective-permute-start(f32[1,1280]{1,0:T(1,128)S(1)} %get-tuple-element.39), channel_id=1, source_target_pairs={{0,1},{1,0},{2,3},{3,2},{4,5},{5,4},{6,7},{7,6},{8,9},{9,8},{10,11... | collective-permute-start | bytes 15368 | tf_op jit(solution)/shard_map/ppermute | solution.py:329
  58.6 10.2 %collective-permute-start.16 = (f32[1,1280]{1,0:T(1,128)S(1)}, f32[1,1280]{1,0:T(1,128)S(1)}, u32[]{:S(2)}, u32[]{:S(2)}) collective-permute-start(f32[1,1280]{1,0:T(1,128)S(1)} %add.16), channel_id=1, source_target_pairs={{0,2},{1,3},{2,0},{3,1},{4,6},{5,7},{6,4},{7,5},{8,10},{9,11},{10,... | collective-permute-start | bytes 15368 | tf_op jit(solution)/shard_map/ppermute | solution.py:329
  68.8 3.7 %collective-permute-start.17 = (f32[1,1280]{1,0:T(1,128)S(1)}, f32[1,1280]{1,0:T(1,128)S(1)}, u32[]{:S(2)}, u32[]{:S(2)}) collective-permute-start(f32[1,1280]{1,0:T(1,128)S(1)} %add.17), channel_id=1, source_target_pairs={{0,4},{4,0},{8,12},{12,8},{16,20},{20,16},{24,28},{28,24},{1,5},{5... | collective-permute-start | bytes 15368 | tf_op jit(solution)/shard_map/ppermute | solution.py:329
  72.5 3.7 %collective-permute-start.18 = (f32[1,1280]{1,0:T(1,128)S(1)}, f32[1,1280]{1,0:T(1,128)S(1)}, u32[]{:S(2)}, u32[]{:S(2)}) collective-permute-start(f32[1,1280]{1,0:T(1,128)S(1)} %add.18), channel_id=1, source_target_pairs={{0,8},{4,12},{8,0},{12,4},{16,24},{20,28},{24,16},{28,20},{1,9},{5... | collective-permute-start | bytes 15368 | tf_op jit(solution)/shard_map/ppermute | solution.py:329
  76.2 4.6 %collective-permute-start.19 = (f32[1,1280]{1,0:T(1,128)S(1)}, f32[1,1280]{1,0:T(1,128)S(1)}, u32[]{:S(2)}, u32[]{:S(2)}) collective-permute-start(f32[1,1280]{1,0:T(1,128)S(1)} %add.19), channel_id=1, source_target_pairs={{0,16},{4,20},{8,24},{12,28},{16,0},{20,4},{24,8},{28,12},{1,17},{... | collective-permute-start | bytes 15368 | tf_op jit(solution)/shard_map/ppermute | solution.py:329
  (6 other events, 6.2 us)
